TPU v7x, 32 devices: a whole 2x2x4 slice. The times are simulated.
32 devices in a mesh: wide: 8 (over z, y), narrow: 4 (over x, core).
Axes of the slice: x: 2, y: 2, z: 4, core: 2. Of those that a mesh axis runs over, the one named last changes fastest.
Arguments:
- values: float32 [512, 16384], P(('wide', 'narrow')), may hold values from -200 to 200, as said below
- cloud_words: int32 [512, 512], P(('wide', 'narrow')), may hold values from -2147483648 to 2147483647, as said below
- history_len: int32 [1], replicated, may hold values from 96 to 256
- monitor_start: int32 [1], replicated, may hold values from 256 to 384
- boundary_table: int32 [512], replicated, may hold values from 500 to 2000
Outputs:
- ratio: float32 [512, 16384], P(('wide', 'narrow'))
- peak_so_far: float32 [512, 16384], P(('wide', 'narrow'))
Inputs may be any that keep to these rules, and one draw needn't show every extreme that they name: `values`: values of an index series, mixed noise and a seasonal cycle of varying scale. `cloud_words`: bit b of word j in the row of date t is 1 when pixel 32 j + b is clear at date t; the first 16 dates are clear for every pixel.
All inputs are finite; a program needn't handle non-finite values.
Results may differ from a plain program's by a relative error of at most 0.0003.
Values sent between devices are 32-bit elements; how exact they have to be, the bound alone decides.
A program may use at most 64 MiB of HBM per device.

v0:
```python
import math
import jax
import jax.numpy as jnp
from jax import lax
from jax.sharding import PartitionSpec as P

PERIOD = 46
HARMONICS = 3
COLS = 8
WINDOW = 64
HIGH = lax.Precision.HIGHEST


def unpack_clear(words):
    shifts = jnp.arange(32, dtype=jnp.int32)
    flags = jnp.bitwise_and(jnp.right_shift(words[:, :, None], shifts[None, None, :]), jnp.int32(1))
    return flags.reshape(words.shape[0], words.shape[1] * 32).astype(jnp.float32)


def harmonic_design(dates):
    day_float = jnp.arange(dates, dtype=jnp.int32).astype(jnp.float32)
    columns = [jnp.ones((dates,), jnp.float32), day_float / dates]
    for harmonic in range(1, HARMONICS + 1):
        phases = 2.0 * math.pi * harmonic / PERIOD * day_float
        columns.append(jnp.cos(phases))
        columns.append(jnp.sin(phases))
    return jnp.stack(columns, axis=1)


def solve_batched(normal_mat, target):
    size_cols = normal_mat.shape[0]
    factor = [[None] * size_cols for row_idx in range(size_cols)]
    for row_idx in range(size_cols):
        for col_idx in range(row_idx + 1):
            summed = normal_mat[row_idx, col_idx]
            for mid_idx in range(col_idx):
                summed = summed - factor[row_idx][mid_idx] * factor[col_idx][mid_idx]
            if row_idx == col_idx:
                factor[row_idx][col_idx] = jnp.sqrt(summed)
            else:
                factor[row_idx][col_idx] = summed / factor[col_idx][col_idx]
    forward = []
    for row_idx in range(size_cols):
        summed = target[row_idx]
        for mid_idx in range(row_idx):
            summed = summed - factor[row_idx][mid_idx] * forward[mid_idx]
        forward.append(summed / factor[row_idx][row_idx])
    solution = [None] * size_cols
    for row_idx in reversed(range(size_cols)):
        summed = forward[row_idx]
        for mid_idx in range(row_idx + 1, size_cols):
            summed = summed - factor[mid_idx][row_idx] * solution[mid_idx]
        solution[row_idx] = summed / factor[row_idx][row_idx]
    return jnp.stack(solution, axis=0)


def fit_statistic(values, clear, history_len, monitor_start, boundary_table):
    dates = values.shape[0]
    day = jnp.arange(dates, dtype=jnp.int32)
    design = harmonic_design(dates)
    in_history = (day < history_len[0]).astype(jnp.float32)[:, None]
    weight = clear * in_history
    outer = (design[:, :, None] * design[:, None, :]).reshape(dates, COLS * COLS)
    normal_mat = jnp.dot(
        outer.T, weight, precision=HIGH, preferred_element_type=jnp.float32
    ).reshape(COLS, COLS, -1)
    target = jnp.dot(design.T, weight * values, precision=HIGH, preferred_element_type=jnp.float32)
    coeffs = solve_batched(normal_mat, target)
    fitted = jnp.dot(design, coeffs, precision=HIGH, preferred_element_type=jnp.float32)
    resid = clear * (values - fitted)
    count = jnp.sum(weight, axis=0)
    squares = jnp.sum(weight * resid * resid, axis=0)
    sigma = jnp.sqrt(squares / (count - COLS) + 1e-06)
    lagged = day[:, None] - day[None, :]
    banded = ((lagged >= 0) & (lagged < WINDOW)).astype(jnp.float32)
    moving = jnp.dot(banded, resid, precision=HIGH, preferred_element_type=jnp.float32)
    scaled = moving / (sigma * jnp.sqrt(count))[None, :]
    bounds = boundary_table.astype(jnp.float32) * 0.001
    watching = (day >= monitor_start[0])[:, None]
    return jnp.where(watching, scaled / bounds[:, None], jnp.float32(0.0))


def per_device(values, cloud_words, history_len, monitor_start, boundary_table):
    arrived = lax.all_to_all(values, ("wide", "narrow"), split_axis=1, concat_axis=0, tiled=True)
    words = lax.all_to_all(cloud_words, ("wide", "narrow"), split_axis=1, concat_axis=0, tiled=True)
    ratio = fit_statistic(arrived, unpack_clear(words), history_len, monitor_start, boundary_table)
    rows = values.shape[0]
    blocks = ratio.reshape(ratio.shape[0] // rows, rows, ratio.shape[1])
    block_peak = lax.cummax(jnp.max(jnp.abs(blocks), axis=1), axis=0)
    earlier = jnp.concatenate([jnp.zeros_like(block_peak[:1]), block_peak[:-1]], axis=0)
    date_ratio = lax.all_to_all(ratio, ("wide", "narrow"), split_axis=0, concat_axis=1, tiled=True)
    before = lax.all_to_all(earlier, ("wide", "narrow"), split_axis=0, concat_axis=1, tiled=True)
    peak = jnp.maximum(lax.cummax(jnp.abs(date_ratio), axis=0), before)
    return (date_ratio, peak)


def solution(mesh):
    placed = (P(("wide", "narrow"), None), P(("wide", "narrow"), None), P(), P(), P())
    return jax.shard_map(
        per_device,
        mesh=mesh,
        in_specs=placed,
        out_specs=(P(("wide", "narrow"), None), P(("wide", "narrow"), None)),
        check_vma=False,
    )
```

profile of v0, /device:TPU:0, one launch (start us, length us, event | category | flops | bytes accessed | tf_op | source)
XLA Modules:
  0.0 92.7 jit_solution(12139132134094349845)
XLA Ops:
  0.6 0.0 copy-start.1
  0.6 1.0 %all_to_all.50 = s32[16,32,16]{2,1,0:T(8,128)S(1)} reshape(s32[16,512]{1,0:T(8,128)} %param.6) | data formatting | bytes 65536 | tf_op jit(solution)/shard_map/all_to_all | solution.py:85
  1.6 0.2 copy.29
  1.8 0.8 reshape.2540
  2.5 7.3 %all-to-all-start = ((s32[32,1,256]{2,1,0:T(1,128)}), s32[32,1,256]{2,1,0:T(1,128)S(1)}, u32[]{:S(2)}, u32[]{:S(2)}) async-start(s32[32,1,256]{2,1,0:T(1,128)} %reshape.2540), calls=%async_computation | async-start | bytes 65536 | tf_op jit(solution)/shard_map/all_to_all | solution.py:85
  9.9 0.1 fusion.93
  11.3 0.1 shift_right_arithmetic.38
  11.4 0.0 copy-done.1
  11.4 1.1 %copy.28 = f32[2,32,8,512]{3,2,0,1:T(8,128)} copy(f32[2,32,8,512]{3,2,1,0:T(8,128)S(1)} %bitcast.435) | data formatting | bytes 2097152 | tf_op jit(solution)/shard_map/all_to_all | solution.py:84
  12.5 0.1 fusion.91
  12.6 4.5 %all-to-all-done = s32[32,1,256]{2,1,0:T(1,128)S(1)} async-done(((s32[32,1,256]{2,1,0:T(1,128)}), s32[32,1,256]{2,1,0:T(1,128)S(1)}, u32[]{:S(2)}, u32[]{:S(2)}) %all-to-all-start) | async-done | bytes 32800 | tf_op jit(solution)/shard_map/all_to_all | solution.py:85
  17.1 2.6 %all-to-all-start.1 = ((f32[16,32,512]{2,0,1:T(8,128)}), f32[16,32,512]{2,0,1:T(8,128)S(1)}, u32[]{:S(2)}, u32[]{:S(2)}) async-start(f32[16,32,512]{2,0,1:T(8,128)} %bitcast.423), calls=%async_computation.1 | async-start | bytes 2097152 | tf_op jit(solution)/shard_map/all_to_all | solution.py:84
  19.8 0.1 fusion.95
  19.9 0.1 convert_multiply_fusion.6
  20.0 0.0 copy-start.2
  20.0 0.7 copy-done.2
  20.7 0.5 broadcast.136
  21.2 0.7 reduce.1
  21.9 0.1 reshape.2541
  22.1 0.1 copy.22
  22.2 0.1 shift_right_arithmetic.35
  22.3 0.3 copy.16
  22.6 0.3 fusion.10
  22.9 0.1 sub.3613
  23.0 0.1 sqrt.482
  23.1 1.1 %fusion.11 = f32[8,8,512]{2,1,0:T(8,128)S(1)} fusion(f32[512,512,1]{0,1,2:T(8,128)S(1)} %bitcast.432, f32[512,8]{0,1:T(8,128)S(1)} %stack.4), kind=kOutput, calls=%fused_computation.20 | convolution fusion | flops 201359360 | bytes 1196032 | tf_op jit(solution)/shard_map/dot_general | solution.py:64
  24.3 21.7 %all-to-all-done.1 = f32[16,32,512]{2,0,1:T(8,128)S(1)} async-done(((f32[16,32,512]{2,0,1:T(8,128)}), f32[16,32,512]{2,0,1:T(8,128)S(1)}, u32[]{:S(2)}, u32[]{:S(2)}) %all-to-all-start.1) | async-done | bytes 1048608 | tf_op jit(solution)/shard_map/all_to_all | solution.py:84
  46.0 0.2 bitcast_multiply_fusion
  46.2 0.6 fusion.121
  46.8 0.2 subtract_divide_fusion.6
  47.0 0.1 rsqrt_multiply_fusion
  47.1 0.2 bitcast_divide_fusion
  47.3 1.3 %fusion.2 = (f32[512]{0:T(512)S(1)}, f32[512,512]{1,0:T(8,128)S(1)}) fusion(s32[512,512]{1,0:T(8,128)S(1)} %copy.16, f32[512]{0:T(512)S(1)} %fusion.96, s32[512]{0:T(512)S(1)} %shift_right_arithmetic.38, f32[512,512]{1,0:T(8,128)S(1)} %bitcast.428, f32[512,8]{0,1:T(8,128)S(1)} %stack.4, f32[8,512]{1,0:T(8,128)S(1)} %stack.5), kind=kOutput, calls=%fused_computation.5 | convolution fusion | flops 27524608 | bytes 3184640 | tf_op jit(solution)/shard_map/dot_general | solution.py:69
  48.6 2.2 %abs_reduce_fusion = (f32[32,512]{1,0:T(8,128)S(1)}, f32[512,512]{1,0:T(8,128)}) fusion(f32[512]{0:T(512)S(1)} %convert_multiply_fusion.2, f32[512]{0:T(512)S(1)} %sqrt_multiply_fusion, f32[512,512]{1,0:T(8,128)S(1)} %get-tuple-element.85, pred[512]{0:T(512)(128)(4,1)S(1)} %iota_compare_fusion.1), kind=kOutput, calls=%fused_computation.8 | convolution fusion | flops 1612955648 | bytes 2167296 | tf_op jit(solution)/shard_map/dot_general | solution.py:76
  50.8 3.5 %all-to-all-start.2 = ((f32[32,16,512]{2,1,0:T(8,128)}), f32[32,16,512]{2,1,0:T(8,128)S(1)}, u32[]{:S(2)}, u32[]{:S(2)}) async-start(f32[32,16,512]{2,1,0:T(8,128)} %bitcast.50), calls=%async_computation.2 | async-start | bytes 2097152 | tf_op jit(solution)/shard_map/all_to_all | solution.py:91
  54.4 0.1 reduce_window_max.21
  54.5 0.7 copy.20
  55.2 25.4 %all-to-all-done.2 = f32[32,16,512]{2,1,0:T(8,128)S(1)} async-done(((f32[32,16,512]{2,1,0:T(8,128)}), f32[32,16,512]{2,1,0:T(8,128)S(1)}, u32[]{:S(2)}, u32[]{:S(2)}) %all-to-all-start.2) | async-done | bytes 1048608 | tf_op jit(solution)/shard_map/all_to_all | solution.py:91
  80.6 3.6 %all-to-all-start.3 = ((f32[32,1,512]{2,1,0:T(1,128)}), f32[32,1,512]{2,1,0:T(1,128)S(1)}, u32[]{:S(2)}, u32[]{:S(2)}) async-start(f32[32,1,512]{2,1,0:T(1,128)} %copy.20), calls=%async_computation.3 | async-start | bytes 131072 | tf_op jit(solution)/shard_map/all_to_all | solution.py:92
  84.2 0.1 copy.25
  84.3 0.0 copy-start
  84.3 0.1 abs.6
  84.4 0.9 copy-done
  85.3 0.9 reduce_window_max.20
  86.2 5.4 %all-to-all-done.3 = f32[32,1,512]{2,1,0:T(1,128)S(1)} async-done(((f32[32,1,512]{2,1,0:T(1,128)}), f32[32,1,512]{2,1,0:T(1,128)S(1)}, u32[]{:S(2)}, u32[]{:S(2)}) %all-to-all-start.3) | async-done | bytes 65568 | tf_op jit(solution)/shard_map/all_to_all | solution.py:92
  91.6 1.1 %broadcast_maximum_fusion = f32[16,16384]{1,0:T(8,128)} fusion(f32[16,16384]{1,0:T(8,128)S(1)} %reduce_window_max.20, f32[16384]{0:T(1024)S(1)} %bitcast.437), kind=kLoop, calls=%fused_computation.16 | loop fusion | flops 262144 | bytes 2162688 | tf_op jit(solution)/shard_map/max | solution.py:93
  (13 shorter events, 0.2 us)
Async XLA Ops:
  0.6 10.8 %copy-start.1 = (f32[16,16384]{1,0:T(8,128)S(1)}, f32[16,16384]{1,0:T(8,128)}, u32[]{:S(2)}) copy-start(f32[16,16384]{1,0:T(8,128)} %param.5) | copy-start | bytes 3145732
  2.5 14.6 %all-to-all-start = ((s32[32,1,256]{2,1,0:T(1,128)}), s32[32,1,256]{2,1,0:T(1,128)S(1)}, u32[]{:S(2)}, u32[]{:S(2)}) async-start(s32[32,1,256]{2,1,0:T(1,128)} %reshape.2540), calls=%async_computation | async-start | bytes 65536 | tf_op jit(solution)/shard_map/all_to_all | solution.py:85
  17.1 28.8 %all-to-all-start.1 = ((f32[16,32,512]{2,0,1:T(8,128)}), f32[16,32,512]{2,0,1:T(8,128)S(1)}, u32[]{:S(2)}, u32[]{:S(2)}) async-start(f32[16,32,512]{2,0,1:T(8,128)} %bitcast.423), calls=%async_computation.1 | async-start | bytes 2097152 | tf_op jit(solution)/shard_map/all_to_all | solution.py:84
  20.0 0.7 copy-start.2
  50.8 29.8 %all-to-all-start.2 = ((f32[32,16,512]{2,1,0:T(8,128)}), f32[32,16,512]{2,1,0:T(8,128)S(1)}, u32[]{:S(2)}, u32[]{:S(2)}) async-start(f32[32,16,512]{2,1,0:T(8,128)} %bitcast.50), calls=%async_computation.2 | async-start | bytes 2097152 | tf_op jit(solution)/shard_map/all_to_all | solution.py:91
  80.6 11.0 %all-to-all-start.3 = ((f32[32,1,512]{2,1,0:T(1,128)}), f32[32,1,512]{2,1,0:T(1,128)S(1)}, u32[]{:S(2)}, u32[]{:S(2)}) async-start(f32[32,1,512]{2,1,0:T(1,128)} %copy.20), calls=%async_computation.3 | async-start | bytes 131072 | tf_op jit(solution)/shard_map/all_to_all | solution.py:92
  84.3 1.0 %copy-start = (f32[32,2,8,512]{3,2,0,1:T(8,128)}, f32[32,2,8,512]{3,2,0,1:T(8,128)S(1)}, u32[]{:S(2)}) copy-start(f32[32,2,8,512]{3,2,0,1:T(8,128)S(1)} %copy.25) | copy-start | bytes 3145732
where the time goes:
time: 93.1 us; the launch traced here: 92.7 us
  waiting for transfers between devices  57 us (61%)
  starting transfers between devices  17.1 us (18%)
  local copies, waits for them, and re-layouts  6.78 us (7%)
  matrix products  5.22 us (6%)
  other arithmetic  4.33 us (5%)
  between operations  2.16 us (2%)
    all_to_all x1, waiting for transfers between devices, per_device(): lax.all_to_all(ratio, ('wide', 'narrow'), split_axis=0, concat_axis=1, ti...  25.4 us
    all_to_all x1, waiting for transfers between devices, per_device(): lax.all_to_all(values, ('wide', 'narrow'), split_axis=1, concat_axis=0, t...  21.7 us
    all_to_all x1, starting transfers between devices, per_device(): lax.all_to_all(cloud_words, ('wide', 'narrow'), split_axis=1, concat_axis...  7.33 us
    all_to_all x1, waiting for transfers between devices, per_device(): lax.all_to_all(earlier, ('wide', 'narrow'), split_axis=0, concat_axis=1,...  5.43 us
    all_to_all x1, waiting for transfers between devices, per_device(): lax.all_to_all(cloud_words, ('wide', 'narrow'), split_axis=1, concat_axis...  4.54 us
    all_to_all x1, starting transfers between devices, per_device(): lax.all_to_all(earlier, ('wide', 'narrow'), split_axis=0, concat_axis=1,...  3.62 us
    all_to_all x1, starting transfers between devices, per_device(): lax.all_to_all(ratio, ('wide', 'narrow'), split_axis=0, concat_axis=1, ti...  3.54 us
    all_to_all x1, starting transfers between devices, per_device(): lax.all_to_all(values, ('wide', 'narrow'), split_axis=1, concat_axis=0, t...  2.65 us
  transfers between devices with their start and end apart: 4, of which 4 were waited for; matrix products, arithmetic and copies ran while one was open for 8% of the time, Pallas kernels for 0%

commit v1 on v0

--- a/solution.py
+++ b/solution.py
@@ -81,7 +81,15 @@
 
 
 def per_device(values, cloud_words, history_len, monitor_start, boundary_table):
-    arrived = lax.all_to_all(values, ("wide", "narrow"), split_axis=1, concat_axis=0, tiled=True)
+    arrived = jnp.concatenate(
+        lax.all_to_all(
+            jnp.stack(jnp.split(values, lax.axis_size(("wide", "narrow")), axis=1)),
+            ("wide", "narrow"),
+            0,
+            0,
+        ),
+        axis=0,
+    )
     words = lax.all_to_all(cloud_words, ("wide", "narrow"), split_axis=1, concat_axis=0, tiled=True)
     ratio = fit_statistic(arrived, unpack_clear(words), history_len, monitor_start, boundary_table)
     rows = values.shape[0]

time: 93.1 us -> 111 us (1.19)
  local copies, waits for them, and re-layouts: 6.78 us -> 25.5 us
  waiting for transfers between devices: 57 us -> 52.5 us
  starting transfers between devices: 17.1 us -> 20.4 us
    unnamed x8 -> x39, local copies, waits for them, and re-layouts: 2.42 us -> 21.5 us
    all_to_all x1, waiting for transfers between devices: 4.54 us -> 0.01 us  [per_device(): lax.all_to_all(cloud_words, ('wide', 'narrow'), split_axis=1, concat_axis...]
    all_to_all x1, starting transfers between devices: 2.65 us -> 5.84 us  [per_device(): lax.all_to_all(jnp.stack(jnp.split(values, lax.axis_size(('wide', 'narrow...]
  transfers between devices with their start and end apart: 4 -> 4, of which waited for: 4 -> 3; matrix products, arithmetic and copies ran while one was open for 8% -> 23% of each run, Pallas kernels for 0% -> 0%
where the time goes in v1:
time: 111 us; the launch traced here: 110 us
  waiting for transfers between devices  52.5 us (47%)
  local copies, waits for them, and re-layouts  25.5 us (23%)
  starting transfers between devices  20.4 us (18%)
  matrix products  5.22 us (5%)
  other arithmetic  4.33 us (4%)
  between operations  2.19 us (2%)
    all_to_all x1, waiting for transfers between devices, per_device(): lax.all_to_all(ratio, ('wide', 'narrow'), split_axis=0, concat_axis=1, ti...  25.4 us
    all_to_all x1, waiting for transfers between devices, per_device(): lax.all_to_all(jnp.stack(jnp.split(values, lax.axis_size(('wide', 'narrow...  21.7 us
    unnamed x39, local copies, waits for them, and re-layouts  21.5 us
    all_to_all x1, starting transfers between devices, per_device(): lax.all_to_all(cloud_words, ('wide', 'narrow'), split_axis=1, concat_axis...  7.33 us
    all_to_all x1, starting transfers between devices, per_device(): lax.all_to_all(jnp.stack(jnp.split(values, lax.axis_size(('wide', 'narrow...  5.84 us
    all_to_all x1, waiting for transfers between devices, per_device(): lax.all_to_all(earlier, ('wide', 'narrow'), split_axis=0, concat_axis=1,...  5.43 us
    all_to_all x1, starting transfers between devices, per_device(): lax.all_to_all(ratio, ('wide', 'narrow'), split_axis=0, concat_axis=1, ti...  3.62 us
    all_to_all x1, starting transfers between devices, per_device(): lax.all_to_all(earlier, ('wide', 'narrow'), split_axis=0, concat_axis=1,...  3.62 us
  transfers between devices with their start and end apart: 4, of which 3 were waited for; matrix products, arithmetic and copies ran while one was open for 23% of the time, Pallas kernels for 0%

profile of v1, /device:TPU:0, one launch (start us, length us, event | category | flops | bytes accessed | tf_op | source)
XLA Modules:
  0.0 110.1 jit_solution(10329535436238484293)
XLA Ops:
  0.6 1.0 all_to_all.39
  1.8 0.8 reshape.2541
  2.5 7.3 %all-to-all-start = ((s32[32,1,256]{2,1,0:T(1,128)}), s32[32,1,256]{2,1,0:T(1,128)S(1)}, u32[]{:S(2)}, u32[]{:S(2)}) async-start(s32[32,1,256]{2,1,0:T(1,128)} %reshape.2541), calls=%async_computation | async-start | bytes 65536 | tf_op jit(solution)/shard_map/all_to_all | solution.py:93
  11.4 0.6 constant_dynamic-update-slice_fusion.31
  12.0 0.6 constant_dynamic-update-slice_fusion.30
  12.6 0.6 constant_dynamic-update-slice_fusion.29
  13.2 0.6 constant_dynamic-update-slice_fusion.28
  13.9 0.6 constant_dynamic-update-slice_fusion.27
  14.5 0.6 constant_dynamic-update-slice_fusion.26
  15.1 0.6 constant_dynamic-update-slice_fusion.25
  15.7 0.6 constant_dynamic-update-slice_fusion.24
  16.3 0.6 constant_dynamic-update-slice_fusion.23
  17.0 0.6 constant_dynamic-update-slice_fusion.22
  17.6 0.6 constant_dynamic-update-slice_fusion.21
  18.2 0.6 constant_dynamic-update-slice_fusion.20
  18.8 0.6 constant_dynamic-update-slice_fusion.19
  19.4 0.6 constant_dynamic-update-slice_fusion.18
  20.0 0.6 constant_dynamic-update-slice_fusion.17
  20.7 0.6 constant_dynamic-update-slice_fusion.16
  21.3 0.6 constant_dynamic-update-slice_fusion.15
  21.9 0.6 constant_dynamic-update-slice_fusion.14
  22.5 0.6 constant_dynamic-update-slice_fusion.13
  23.1 0.6 constant_dynamic-update-slice_fusion.12
  23.7 0.6 constant_dynamic-update-slice_fusion.11
  24.4 0.6 constant_dynamic-update-slice_fusion.10
  25.0 0.6 constant_dynamic-update-slice_fusion.9
  25.6 0.6 constant_dynamic-update-slice_fusion.8
  26.2 0.6 constant_dynamic-update-slice_fusion.7
  26.8 0.6 constant_dynamic-update-slice_fusion.6
  27.4 0.6 constant_dynamic-update-slice_fusion.5
  28.1 0.6 constant_dynamic-update-slice_fusion.4
  28.7 0.6 constant_dynamic-update-slice_fusion.3
  29.3 0.6 constant_dynamic-update-slice_fusion.2
  31.3 5.8 %all-to-all-start.1 = ((f32[32,16,512]{2,1,0:T(8,128)}), f32[32,16,512]{2,1,0:T(8,128)S(1)}, u32[]{:S(2)}, u32[]{:S(2)}) async-start(f32[32,16,512]{2,1,0:T(8,128)} %constant_dynamic-update-slice_fusion), calls=%async_computation.1 | async-start | bytes 2097152 | tf_op jit(solution)/shard_map/all_to_all | solution.py:85
  37.4 0.7 copy-done.2
  38.6 0.7 reduce.1
  40.4 1.1 %fusion.11 = f32[8,8,512]{2,1,0:T(8,128)S(1)} fusion(f32[512,512,1]{0,1,2:T(8,128)S(1)} %bitcast.490, f32[512,8]{0,1:T(8,128)S(1)} %stack.153), kind=kOutput, calls=%fused_computation.19 | convolution fusion | flops 201359360 | bytes 1196032 | tf_op jit(solution)/shard_map/dot_general | solution.py:64
  41.7 21.7 %all-to-all-done.1 = f32[32,16,512]{2,1,0:T(8,128)S(1)} async-done(((f32[32,16,512]{2,1,0:T(8,128)}), f32[32,16,512]{2,1,0:T(8,128)S(1)}, u32[]{:S(2)}, u32[]{:S(2)}) %all-to-all-start.1) | async-done | bytes 1048608 | tf_op jit(solution)/shard_map/all_to_all | solution.py:85
  64.7 1.3 %fusion.2 = (f32[512]{0:T(512)S(1)}, f32[512,512]{1,0:T(8,128)S(1)}) fusion(s32[512,512]{1,0:T(8,128)S(1)} %copy.14, f32[512]{0:T(512)S(1)} %fusion.96, s32[512]{0:T(512)S(1)} %shift_right_arithmetic.38, f32[512,512]{1,0:T(8,128)S(1)} %bitcast.486, f32[512,8]{0,1:T(8,128)S(1)} %stack.153, f32[8,512]{1,0:T(8,128)S(1)} %stack.154), kind=kOutput, calls=%fused_computation.5 | convolution fusion | flops 27524608 | bytes 3184640 | tf_op jit(solution)/shard_map/dot_general | solution.py:69
  66.0 2.2 %abs_reduce_fusion = (f32[32,512]{1,0:T(8,128)S(1)}, f32[512,512]{1,0:T(8,128)}) fusion(f32[512]{0:T(512)S(1)} %convert_multiply_fusion.2, f32[512]{0:T(512)S(1)} %sqrt_multiply_fusion, f32[512,512]{1,0:T(8,128)S(1)} %get-tuple-element.85, pred[512]{0:T(512)(128)(4,1)S(1)} %iota_compare_fusion.1), kind=kOutput, calls=%fused_computation.7 | convolution fusion | flops 1612955648 | bytes 2167296 | tf_op jit(solution)/shard_map/dot_general | solution.py:76
  68.2 3.6 %all-to-all-start.2 = ((f32[32,16,512]{2,1,0:T(8,128)}), f32[32,16,512]{2,1,0:T(8,128)S(1)}, u32[]{:S(2)}, u32[]{:S(2)}) async-start(f32[32,16,512]{2,1,0:T(8,128)} %bitcast.80), calls=%async_computation.2 | async-start | bytes 2097152 | tf_op jit(solution)/shard_map/all_to_all | solution.py:99
  71.9 0.7 copy.17
  72.6 25.4 %all-to-all-done.2 = f32[32,16,512]{2,1,0:T(8,128)S(1)} async-done(((f32[32,16,512]{2,1,0:T(8,128)}), f32[32,16,512]{2,1,0:T(8,128)S(1)}, u32[]{:S(2)}, u32[]{:S(2)}) %all-to-all-start.2) | async-done | bytes 1048608 | tf_op jit(solution)/shard_map/all_to_all | solution.py:99
  98.0 3.6 %all-to-all-start.3 = ((f32[32,1,512]{2,1,0:T(1,128)}), f32[32,1,512]{2,1,0:T(1,128)S(1)}, u32[]{:S(2)}, u32[]{:S(2)}) async-start(f32[32,1,512]{2,1,0:T(1,128)} %copy.17), calls=%async_computation.3 | async-start | bytes 131072 | tf_op jit(solution)/shard_map/all_to_all | solution.py:100
  101.8 0.9 copy-done
  102.7 0.9 reduce_window_max.20
  103.6 5.4 %all-to-all-done.3 = f32[32,1,512]{2,1,0:T(1,128)S(1)} async-done(((f32[32,1,512]{2,1,0:T(1,128)}), f32[32,1,512]{2,1,0:T(1,128)S(1)}, u32[]{:S(2)}, u32[]{:S(2)}) %all-to-all-start.3) | async-done | bytes 65568 | tf_op jit(solution)/shard_map/all_to_all | solution.py:100
  109.1 1.1 broadcast_maximum_fusion
  (42 shorter events, 5.2 us)
Async XLA Ops:
  0.6 10.8 %copy-start.1 = (f32[16,16384]{1,0:T(8,128)S(1)}, f32[16,16384]{1,0:T(8,128)}, u32[]{:S(2)}) copy-start(f32[16,16384]{1,0:T(8,128)} %param.5) | copy-start | bytes 3145732
  2.5 28.7 %all-to-all-start = ((s32[32,1,256]{2,1,0:T(1,128)}), s32[32,1,256]{2,1,0:T(1,128)S(1)}, u32[]{:S(2)}, u32[]{:S(2)}) async-start(s32[32,1,256]{2,1,0:T(1,128)} %reshape.2541), calls=%async_computation | async-start | bytes 65536 | tf_op jit(solution)/shard_map/all_to_all | solution.py:93
  31.3 32.1 %all-to-all-start.1 = ((f32[32,16,512]{2,1,0:T(8,128)}), f32[32,16,512]{2,1,0:T(8,128)S(1)}, u32[]{:S(2)}, u32[]{:S(2)}) async-start(f32[32,16,512]{2,1,0:T(8,128)} %constant_dynamic-update-slice_fusion), calls=%async_computation.1 | async-start | bytes 2097152 | tf_op jit(solution)/shard_map/all_to_all | solution.py:85
  37.4 0.7 copy-start.2
  68.2 29.8 %all-to-all-start.2 = ((f32[32,16,512]{2,1,0:T(8,128)}), f32[32,16,512]{2,1,0:T(8,128)S(1)}, u32[]{:S(2)}, u32[]{:S(2)}) async-start(f32[32,16,512]{2,1,0:T(8,128)} %bitcast.80), calls=%async_computation.2 | async-start | bytes 2097152 | tf_op jit(solution)/shard_map/all_to_all | solution.py:99
  98.0 11.0 %all-to-all-start.3 = ((f32[32,1,512]{2,1,0:T(1,128)}), f32[32,1,512]{2,1,0:T(1,128)S(1)}, u32[]{:S(2)}, u32[]{:S(2)}) async-start(f32[32,1,512]{2,1,0:T(1,128)} %copy.17), calls=%async_computation.3 | async-start | bytes 131072 | tf_op jit(solution)/shard_map/all_to_all | solution.py:100
  101.7 1.0 copy-start
